TPU v7x, 256 devices: a whole 4x4x8 slice. The times are simulated.
256 devices in a mesh: expert: 64 (over x, z, core), tensor: 4 (over y).
Axes of the slice: x: 4, y: 4, z: 8, core: 2. Of those that a mesh axis runs over, the one named last changes fastest.
Arguments:
- tokens: bfloat16 [8192, 3584], P('expert', 'tensor'), may hold values from -6 to 6
- expert_ids: int32 [8192, 4], P('expert'), may hold values from 0 to 63, all different within a row; in each aligned block of 128 rows (0 to 127, 128 to 255, ...) at most 12 rows name the same one
- gate_values: bfloat16 [8192, 4], P('expert'), may hold values from 0.049804688 to 0.3984375
- w_gate: bfloat16 [64, 3584, 1024], P('expert', None, 'tensor'), may hold values from -0.09375 to 0.09375
- w_up: bfloat16 [64, 3584, 1024], P('expert', None, 'tensor'), may hold values from -0.09375 to 0.09375
- w_down: bfloat16 [64, 1024, 3584], P('expert', 'tensor'), may hold values from -0.1875 to 0.1875
- shared_gate: bfloat16 [3584, 1024], P(None, 'tensor'), may hold values from -0.09375 to 0.09375
- shared_up: bfloat16 [3584, 1024], P(None, 'tensor'), may hold values from -0.09375 to 0.09375
- shared_down: bfloat16 [1024, 3584], P('tensor'), may hold values from -0.1875 to 0.1875
Outputs:
- moe_output: bfloat16 [8192, 3584], P('expert', 'tensor')
Inputs may be any that keep to these rules, and one draw needn't show every extreme that they name: `expert_ids`: each token names 4 different experts. Among the 128 tokens of one index of the expert axis (aligned blocks of 128 rows) no expert is named by more than 12 tokens, a bound that some block reaches.
All inputs are finite; a program needn't handle non-finite values.
Results may differ from a plain program's by a relative error of at most 0.013.
Values may be sent and summed in bfloat16 or wider, within the bound.
No kernel may reach another device: no remote copies, remote signals or barrier semaphores. Data moves between devices by JAX's collectives and lax.ppermute only.
A program may use at most 64 MiB of HBM per device.

v0:
```python
import jax
import jax.numpy as jnp
from jax import lax
from jax.sharding import Mesh
from jax.sharding import PartitionSpec as P

EXPERT = ("expert_0", "expert_1", "expert_2")


def in_order(tiles, dim):
    shape = list(tiles.shape[1:])
    shape[dim] *= tiles.shape[0]
    return jnp.moveaxis(tiles, 0, dim).reshape(shape)


def from_everyone(x, axis):
    copies = jnp.broadcast_to(x, (lax.axis_size(axis), *x.shape))
    return lax.all_to_all(copies, axis, split_axis=0, concat_axis=0, tiled=True)


def collect(x, axis, dim):
    return in_order(from_everyone(x, axis), dim)


def in_blocks(x, dim, devices):
    before, after = (x.shape[:dim], x.shape[dim + 1 :])
    return jnp.moveaxis(x.reshape(*before, devices, -1, *after), dim, 0)


def sent_and_summed(x, axis, dim):
    tiles = in_blocks(x, dim, lax.axis_size(axis))
    arrived = lax.all_to_all(tiles, axis, split_axis=0, concat_axis=0, tiled=True)
    return arrived.astype(jnp.float32).sum(axis=0)


def turned_blocks(tiles, axes, sequence):
    shape = [lax.axis_size(a) for a in axes]
    tiles = tiles.reshape(*shape, *tiles.shape[1:])
    for k in sequence:
        tiles = lax.all_to_all(tiles, axes[k], split_axis=k, concat_axis=k, tiled=True)
    return tiles.reshape(-1, *tiles.shape[len(axes) :])


def core_and_chips(x, groups, sequence, split_dim, concat_dim):
    devices = lax.axis_size(groups[0]) * lax.axis_size(groups[1])
    tiles = in_blocks(x, split_dim, devices)
    return in_order(turned_blocks(tiles, groups, sequence), concat_dim)


def per_device(
    tokens, expert_ids, gate_values, w_gate, w_up, w_down, shared_gate, shared_up, shared_down
):
    tok_dev, narrow = tokens.shape
    top_count = expert_ids.shape[1]
    per_lane, features, quarter = w_gate.shape
    lane_count = lax.axis_size(EXPERT)
    experts_all = lane_count * per_lane
    capacity = min(tok_dev, 3 * tok_dev * top_count // (2 * experts_all))
    total_rows = experts_all * capacity
    numbers = jnp.arange(experts_all, dtype=jnp.int32)
    onehot = (expert_ids[:, :, None] == numbers).astype(jnp.int32)
    per_token = jnp.sum(onehot, axis=1)
    earlier = jnp.cumsum(per_token, axis=0) - per_token
    slot_index = jnp.sum(onehot * earlier[:, None, :], axis=2)
    target = expert_ids * capacity + slot_index
    token_index = jnp.repeat(jnp.arange(tok_dev, dtype=jnp.int32), top_count)
    owners = jnp.full((total_rows,), tok_dev, jnp.int32).at[target.reshape(-1)].set(token_index)
    features_all = collect(tokens, "tensor", 1)
    shared_gate_sums = jnp.dot(features_all, shared_gate, preferred_element_type=jnp.float32)
    shared_up_sums = jnp.dot(features_all, shared_up, preferred_element_type=jnp.float32)
    shared_hidden = (jax.nn.silu(shared_gate_sums) * shared_up_sums).astype(jnp.bfloat16)
    shared_partial = jnp.dot(shared_hidden, shared_down, preferred_element_type=jnp.float32)
    padded = jnp.concatenate([tokens, jnp.zeros((1, narrow), jnp.bfloat16)], axis=0)
    outgoing = padded[owners].reshape(lane_count, per_lane * capacity, narrow)
    arrived = lax.all_to_all(outgoing, EXPERT, split_axis=0, concat_axis=0, tiled=True)
    arrived = arrived.reshape(lane_count, per_lane, capacity, narrow)
    block_rows = lax.all_gather(arrived, "tensor", axis=3, tiled=True)
    gate_more = jnp.einsum("sjcd,jdf->sjcf", block_rows, w_gate, preferred_element_type=jnp.float32)
    up_more = jnp.einsum("sjcd,jdf->sjcf", block_rows, w_up, preferred_element_type=jnp.float32)
    hidden = (jax.nn.silu(gate_more) * up_more).astype(jnp.bfloat16)
    partial_value = jnp.einsum("sjcf,jfd->sjcd", hidden, w_down, preferred_element_type=jnp.float32)
    summed = sent_and_summed(partial_value.astype(jnp.bfloat16), "tensor", 3)
    returned = core_and_chips(
        summed.reshape(lane_count, per_lane * capacity, narrow).astype(jnp.bfloat16),
        (("expert_0", "expert_1"), "expert_2"),
        (1, 0),
        0,
        0,
    ).astype(jnp.float32)
    picked = returned.reshape(total_rows, narrow)[target]
    routed = jnp.sum(gate_values.astype(jnp.float32)[:, :, None] * picked, axis=1)
    shared_total = sent_and_summed(shared_partial.astype(jnp.bfloat16), "tensor", 1)
    return (routed + shared_total).astype(jnp.bfloat16)


def solution(mesh):
    torus = Mesh(
        mesh.devices.reshape(4, 8, 2, mesh.shape["tensor"]),
        ("expert_0", "expert_1", "expert_2", "tensor"),
    )
    placed = (
        P(EXPERT, "tensor"),
        P(EXPERT, None),
        P(EXPERT, None),
        P(EXPERT, None, "tensor"),
        P(EXPERT, None, "tensor"),
        P(EXPERT, "tensor", None),
        P(None, "tensor"),
        P(None, "tensor"),
        P("tensor", None),
    )
    return jax.shard_map(
        per_device, mesh=torus, in_specs=placed, out_specs=P(EXPERT, "tensor"), check_vma=False
    )
```

profile of v0, /device:TPU:32, one launch (start us, length us, event | category | flops | bytes accessed | tf_op | source)
XLA Modules:
  0.0 321.1 jit_solution(12613605834629810689)
XLA Ops:
  6.5 0.8 convert_reduce_fusion.1
  7.4 0.1 copy.45
  7.5 0.2 reduce_window_sum.11
  7.7 0.1 copy.47
  7.7 0.7 select_reduce_fusion
  8.5 0.7 compare_select_fusion.2
  9.1 0.1 copy.48
  9.3 0.1 reshape.98
  9.4 0.1 reshape.131
  9.5 2.4 scatter_custom_fusion
  12.0 1.0 concatenate.3
  12.9 2.8 gather_fusion
  15.8 1.4 reshape.100
  17.2 56.0 %all_to_all.30 = bf16[64,12,896]{2,1,0:T(8,128)(2,1)S(1)} all-to-all(bf16[64,12,896]{2,1,0:T(8,128)(2,1)} %reshape.100), channel_id=1, replica_groups=mesh['expert_0'=4,'expert_1'=8,'expert_2'=2,'tensor'=4] {'expert_0','exp..., dimensions={0} | all-to-all | bytes 2752512 | tf_op jit(solution)/shard_map/all_to_all | solution.py:75
  73.2 1.4 copy.49
  74.6 0.0 all-gather.3.cloned.1.call-update
  74.7 0.2 copy.57
  74.9 1.1 broadcast_in_dim.25
  75.9 4.5 %all-to-all-start.4 = ((bf16[4,128,896]{1,2,0:T(8,128)(2,1)}), bf16[4,128,896]{1,2,0:T(8,128)(2,1)S(1)}, u32[]{:S(2)}, u32[]{:S(2)}) async-start(bf16[4,128,896]{1,2,0:T(8,128)(2,1)} %broadcast_in_dim.25), calls=%async_computation.4 | async-start | bytes 1835008 | tf_op jit(solution)/shard_map/all_to_all | solution.py:18
  80.4 58.3 %all-gather.3.cloned.1.call-done = bf16[64,12,3584]{2,0,1:T(8,128)(2,1)} async-done(((bf16[64,12,896]{2,0,1:T(8,128)(2,1)}), bf16[64,12,3584]{2,0,1:T(8,128)(2,1)}) %all-gather.3.cloned.1.call-update) | async-done | bytes 5505040 | tf_op jit(solution)/shard_map/all_gather | solution.py:77
  138.6 5.6 %fusion.5 = f32[64,1,12,256]{3,0,2,1:T(8,128)} fusion(bf16[64,12,3584]{2,0,1:T(8,128)(2,1)} %all-gather.3.cloned.1.call-done, bf16[1,3584,256]{2,1,0:T(8,128)(2,1)} %param.12), kind=kOutput, calls=%fused_computation.14 | convolution fusion | flops 1409286144 | bytes 8126464 | tf_op jit(solution)/shard_map/sjcd,jdf->sjcf/dot_general | solution.py:78
  144.3 11.5 %convolution_convert_fusion = bf16[64,12,3584]{2,0,1:T(8,128)(2,1)} fusion(bf16[1,256,3584]{2,1,0:T(8,128)(2,1)S(1)} %copy-done, bf16[64,12,3584]{2,0,1:T(8,128)(2,1)} %all-gather.3.cloned.1.call-done, bf16[1,3584,256]{2,1,0:T(8,128)(2,1)} %param.13, f32[64,1,12,256]{3,0,2,1:T(8,128)} %fusion.5), kind=kOutput, calls=%fused_computation.3 | convolution fusion | flops 2822504448 | bytes 15466496 | tf_op jit(solution)/shard_map/sjcf,jfd->sjcd/dot_general | solution.py:81
  155.7 5.8 %copy.65 = bf16[1,12,8,4,8,896]{5,4,2,1,0,3:T(8,128)(2,1)} copy(bf16[1,12,8,4,8,896]{5,4,3,2,1,0:T(8,128)(2,1)} %bitcast.85) | data formatting | bytes 11010048 | tf_op jit(solution)/shard_map/reshape | solution.py:27
  161.6 5.4 %all-to-all-start.1 = ((bf16[4,64,1,12,896]{4,1,3,2,0:T(8,128)(2,1)}), bf16[4,64,1,12,896]{4,1,3,2,0:T(8,128)(2,1)}, u32[]{:S(2)}, u32[]{:S(2)}) async-start(bf16[4,64,1,12,896]{4,1,3,2,0:T(8,128)(2,1)} %bitcast.82), calls=%async_computation.1 | async-start | bytes 11010048 | tf_op jit(solution)/shard_map/all_to_all | solution.py:32
  167.0 0.5 fusion.39
  167.5 3.3 %convolution_convert_fusion.1 = bf16[128,3584]{1,0:T(8,128)(2,1)S(1)} fusion(bf16[256,3584]{1,0:T(8,128)(2,1)} %param.17, bf16[128,3584]{0,1:T(8,128)(2,1)S(1)} %bitcast.84, bf16[3584,256]{1,0:T(8,128)(2,1)} %param.16, f32[128,256]{1,0:T(8,128)S(1)} %fusion.39), kind=kOutput, calls=%fused_computation.5 | convolution fusion | flops 470417408 | bytes 5636096 | tf_op jit(solution)/shard_map/dot_general | solution.py:72
  170.8 1.0 copy.66
  171.8 58.3 %all-to-all-done.1 = bf16[4,64,1,12,896]{4,1,3,2,0:T(8,128)(2,1)} async-done(((bf16[4,64,1,12,896]{4,1,3,2,0:T(8,128)(2,1)}), bf16[4,64,1,12,896]{4,1,3,2,0:T(8,128)(2,1)}, u32[]{:S(2)}, u32[]{:S(2)}) %all-to-all-start.1) | async-done | bytes 5505056 | tf_op jit(solution)/shard_map/all_to_all | solution.py:32
  230.1 3.6 %reduce_sum.50 = bf16[64,12,896]{2,0,1:T(8,128)(2,1)S(1)} reduce(bf16[4,64,1,12,896]{4,1,3,2,0:T(8,128)(2,1)} %all-to-all-done.1, bf16[]{:T(256)} %constant.8.clone.1), dimensions={0,2}, to_apply=%region_4.5 | reduce | flops 2064384 | bytes 6881282 | tf_op jit(solution)/shard_map/reduce_sum | solution.py:33
  233.7 0.6 convert_element_type.59
  234.3 0.2 copy.52
  234.5 4.8 %all_to_all.31 = bf16[32,2,1,12,896]{4,0,3,2,1:T(8,128)(2,1)S(1)} all-to-all(bf16[32,2,1,12,896]{4,0,3,2,1:T(8,128)(2,1)S(1)} %copy.52), channel_id=1, replica_groups=mesh['expert_0'=4,'expert_1'=8,'expert_2'=2,'tensor'=4] {'expert_2'}, dimensions={1} | all-to-all | bytes 2752512 | tf_op jit(solution)/shard_map/all_to_all | solution.py:40
  239.3 3.5 %all-to-all-start.5 = ((bf16[4,128,896]{2,1,0:T(8,128)(2,1)}), bf16[4,128,896]{2,1,0:T(8,128)(2,1)S(1)}, u32[]{:S(2)}, u32[]{:S(2)}) async-start(bf16[4,128,896]{2,1,0:T(8,128)(2,1)} %bitcast.81), calls=%async_computation.5 | async-start | bytes 1835008 | tf_op jit(solution)/shard_map/all_to_all | solution.py:32
  242.8 2.5 copy.53
  245.3 11.7 %all-to-all-done.5 = bf16[4,128,896]{2,1,0:T(8,128)(2,1)S(1)} async-done(((bf16[4,128,896]{2,1,0:T(8,128)(2,1)}), bf16[4,128,896]{2,1,0:T(8,128)(2,1)S(1)}, u32[]{:S(2)}, u32[]{:S(2)}) %all-to-all-start.5) | async-done | bytes 917536 | tf_op jit(solution)/shard_map/all_to_all | solution.py:32
  257.1 6.9 %all-to-all-start.3 = ((bf16[32,2,1,12,896]{4,1,3,2,0:T(2,128)(2,1)}), bf16[32,2,1,12,896]{4,1,3,2,0:T(2,128)(2,1)S(1)}, u32[]{:S(2)}, u32[]{:S(2)}) async-start(bf16[32,2,1,12,896]{4,1,3,2,0:T(2,128)(2,1)} %copy.53), calls=%async_computation.3 | async-start | bytes 2752512 | tf_op jit(solution)/shard_map/all_to_all | solution.py:40
  263.9 0.1 copy.56
  264.0 0.1 reshape.121
  264.2 0.1 copy.44
  264.3 0.1 convert_reduce_fusion
  264.4 34.2 %all-to-all-done.3 = bf16[32,2,1,12,896]{4,1,3,2,0:T(2,128)(2,1)S(1)} async-done(((bf16[32,2,1,12,896]{4,1,3,2,0:T(2,128)(2,1)}), bf16[32,2,1,12,896]{4,1,3,2,0:T(2,128)(2,1)S(1)}, u32[]{:S(2)}, u32[]{:S(2)}) %all-to-all-start.3) | async-done | bytes 1376288 | tf_op jit(solution)/shard_map/all_to_all | solution.py:40
  298.6 0.3 copy_convert_fusion
  299.0 3.4 %copy.55 = f32[32,2,1,12,896]{4,3,1,0,2:T(8,128)} copy(f32[32,2,1,12,896]{4,0,3,2,1:T(8,128)S(1)} %copy_convert_fusion) | data formatting | bytes 5505024 | tf_op jit(solution)/shard_map/convert_element_type | solution.py:89
  302.4 2.9 reshape.110
  305.3 2.7 gather_fusion.1
  307.9 2.9 reshape.120
  310.9 2.7 multiply_reduce_fusion
  313.6 0.7 add_convert_fusion
  (18 shorter events, 0.1 us)
Async XLA Ops:
  6.5 137.7 %copy-start = (bf16[1,256,3584]{2,1,0:T(8,128)(2,1)S(1)}, bf16[1,256,3584]{2,1,0:T(8,128)(2,1)}, u32[]{:S(2)}) copy-start(bf16[1,256,3584]{2,1,0:T(8,128)(2,1)} %param.14) | copy-start | bytes 5505028
  6.5 132.1 %all-gather.3.cloned.1.call-start = ((), (), s32[]{:S(2)}) async-start(), calls=%async_computation.6 | async-start | bytes 6881280 | tf_op jit(solution)/shard_map/all_gather | solution.py:77
  73.2 1.4 copy-start.3
  75.9 85.7 %all-to-all-start.4 = ((bf16[4,128,896]{1,2,0:T(8,128)(2,1)}), bf16[4,128,896]{1,2,0:T(8,128)(2,1)S(1)}, u32[]{:S(2)}, u32[]{:S(2)}) async-start(bf16[4,128,896]{1,2,0:T(8,128)(2,1)} %broadcast_in_dim.25), calls=%async_computation.4 | async-start | bytes 1835008 | tf_op jit(solution)/shard_map/all_to_all | solution.py:18
  161.6 5.5 %copy-start.2 = (bf16[3584,256]{1,0:T(8,128)(2,1)S(1)}, bf16[3584,256]{1,0:T(8,128)(2,1)}, u32[]{:S(2)}) copy-start(bf16[3584,256]{1,0:T(8,128)(2,1)} %param.15) | copy-start | bytes 5505028
  161.6 68.5 %all-to-all-start.1 = ((bf16[4,64,1,12,896]{4,1,3,2,0:T(8,128)(2,1)}), bf16[4,64,1,12,896]{4,1,3,2,0:T(8,128)(2,1)}, u32[]{:S(2)}, u32[]{:S(2)}) async-start(bf16[4,64,1,12,896]{4,1,3,2,0:T(8,128)(2,1)} %bitcast.82), calls=%async_computation.1 | async-start | bytes 11010048 | tf_op jit(solution)/shard_map/all_to_all | solution.py:32
  239.3 17.7 %all-to-all-start.5 = ((bf16[4,128,896]{2,1,0:T(8,128)(2,1)}), bf16[4,128,896]{2,1,0:T(8,128)(2,1)S(1)}, u32[]{:S(2)}, u32[]{:S(2)}) async-start(bf16[4,128,896]{2,1,0:T(8,128)(2,1)} %bitcast.81), calls=%async_computation.5 | async-start | bytes 1835008 | tf_op jit(solution)/shard_map/all_to_all | solution.py:32
  245.3 18.8 %copy-start.4 = (bf16[128,4]{0,1:T(4,128)(2,1)S(1)}, bf16[128,4]{0,1:T(4,128)(2,1)}, u32[]{:S(2)}) copy-start(bf16[128,4]{0,1:T(4,128)(2,1)} %param.11) | copy-start | bytes 3076
  257.1 41.6 %all-to-all-start.3 = ((bf16[32,2,1,12,896]{4,1,3,2,0:T(2,128)(2,1)}), bf16[32,2,1,12,896]{4,1,3,2,0:T(2,128)(2,1)S(1)}, u32[]{:S(2)}, u32[]{:S(2)}) async-start(bf16[32,2,1,12,896]{4,1,3,2,0:T(2,128)(2,1)} %copy.53), calls=%async_computation.3 | async-start | bytes 2752512 | tf_op jit(solution)/shard_map/all_to_all | solution.py:40
  307.9 6.4 %copy-start.1 = (bf16[1,256,3584]{2,1,0:T(8,128)(2,1)S(1)}, bf16[1,256,3584]{2,1,0:T(8,128)(2,1)}, u32[]{:S(2)}) copy-start(bf16[1,256,3584]{2,1,0:T(8,128)(2,1)} %param.14) | copy-start | bytes 5505028
Sparse Core Ops, SparseCore 0:
  74.8 63.8 all-gather.2
where the time goes:
time: 322 us; the launch traced here: 321 us
  waiting for transfers between devices  163 us (51%)
  blocking collectives  60.9 us (19%)
  local copies, waits for them, and re-layouts  33.1 us (10%)
  matrix products  20.8 us (6%)
  starting transfers between devices  20.3 us (6%)
  between operations  13.6 us (4%)
  other arithmetic  9.92 us (3%)
    all_to_all x2, waiting for transfers between devices, sent_and_summed(): lax.all_to_all(tiles, axis, split_axis=0, concat_axis=0, tiled=True)  70.1 us
    all_gather x1, waiting for transfers between devices, per_device(): block_rows = lax.all_gather(arrived, 'tensor', axis=3, tiled=True)  58.3 us
    all_to_all x1, blocking collectives, per_device(): lax.all_to_all(outgoing, EXPERT, split_axis=0, concat_axis=0, tiled=True)  56 us
    all_to_all x1, waiting for transfers between devices, turned_blocks(): lax.all_to_all(tiles, axes[k], split_axis=k, concat_axis=k, tiled=True)  34.2 us
    dot_general x1, matrix products, per_device(): jnp.einsum('sjcf,jfd->sjcd', hidden, w_down, preferred_element_type=jnp.f...  11.5 us
    all_to_all x2, starting transfers between devices, sent_and_summed(): lax.all_to_all(tiles, axis, split_axis=0, concat_axis=0, tiled=True)  8.94 us
    all_to_all x1, starting transfers between devices, turned_blocks(): lax.all_to_all(tiles, axes[k], split_axis=k, concat_axis=k, tiled=True)  6.87 us
    reshape x2, local copies, waits for them, and re-layouts, in_blocks(): return jnp.moveaxis(x.reshape(*before, devices, -1, *after), dim, 0)  6.86 us
  transfers between devices with their start and end apart: 5, of which 4 were waited for; matrix products, arithmetic and copies ran while one was open for 10% of the time, Pallas kernels for 0%

commit v1 on v0

--- a/solution.py
+++ b/solution.py
@@ -74,7 +74,11 @@
     outgoing = padded[owners].reshape(lane_count, per_lane * capacity, narrow)
     arrived = lax.all_to_all(outgoing, EXPERT, split_axis=0, concat_axis=0, tiled=True)
     arrived = arrived.reshape(lane_count, per_lane, capacity, narrow)
-    block_rows = lax.all_gather(arrived, "tensor", axis=3, tiled=True)
+    length = lax.axis_size("tensor")
+    repeats = [length if d == 3 else 1 for d in range(arrived.ndim)]
+    block_rows = lax.all_to_all(
+        jnp.tile(arrived, repeats), "tensor", split_axis=3, concat_axis=3, tiled=True
+    )
     gate_more = jnp.einsum("sjcd,jdf->sjcf", block_rows, w_gate, preferred_element_type=jnp.float32)
     up_more = jnp.einsum("sjcd,jdf->sjcf", block_rows, w_up, preferred_element_type=jnp.float32)
     hidden = (jax.nn.silu(gate_more) * up_more).astype(jnp.bfloat16)

time: 322 us -> 373 us (1.16)
  local copies, waits for them, and re-layouts: 33.1 us -> 87.3 us
  between operations: 13.6 us -> 0.22 us
  starting transfers between devices: 20.3 us -> 25 us
  waiting for transfers between devices: 163 us -> 167 us
    all_to_all x0 -> x1, waiting for transfers between devices: none -> 63.3 us  [per_device(): lax.all_to_all(jnp.tile(arrived, repeats), 'tensor', split_axis=3, concat...]
    all_gather x1 -> x0, waiting for transfers between devices: 58.3 us -> none  [per_device(): block_rows = lax.all_gather(arrived, 'tensor', axis=3, tiled=True)]
    unnamed x11 -> x13, local copies, waits for them, and re-layouts: 0.19 us -> 23.6 us
    all_to_all x0 -> x1, local copies, waits for them, and re-layouts: none -> 15.6 us  [per_device(): lax.all_to_all(jnp.tile(arrived, repeats), 'tensor', split_axis=3, concat...]
    another operation x0 -> x1, local copies, waits for them, and re-layouts: none -> 8.58 us  [per_device(): jnp.tile(arrived, repeats)]
    all_to_all x1, local copies, waits for them, and re-layouts: 1.42 us -> 8.03 us  [per_device(): lax.all_to_all(outgoing, EXPERT, split_axis=0, concat_axis=0, tiled=True)]
    all_to_all x0 -> x1, starting transfers between devices: none -> 5.25 us  [per_device(): lax.all_to_all(jnp.tile(arrived, repeats), 'tensor', split_axis=3, concat...]
  transfers between devices with their start and end apart: 5 -> 5, of which waited for: 4 -> 4; matrix products, arithmetic and copies ran while one was open for 10% -> 16% of each run, Pallas kernels for 0% -> 0%
where the time goes in v1:
time: 373 us; the launch traced here: 371 us
  waiting for transfers between devices  167 us (45%)
  local copies, waits for them, and re-layouts  87.3 us (23%)
  blocking collectives  61 us (16%)
  starting transfers between devices  25 us (7%)
  matrix products  20.8 us (6%)
  other arithmetic  9.92 us (3%)
    all_to_all x2, waiting for transfers between devices, sent_and_summed(): lax.all_to_all(tiles, axis, split_axis=0, concat_axis=0, tiled=True)  69.3 us
    all_to_all x1, waiting for transfers between devices, per_device(): lax.all_to_all(jnp.tile(arrived, repeats), 'tensor', split_axis=3, concat...  63.3 us
    all_to_all x1, blocking collectives, per_device(): lax.all_to_all(outgoing, EXPERT, split_axis=0, concat_axis=0, tiled=True)  56.1 us
    all_to_all x1, waiting for transfers between devices, turned_blocks(): lax.all_to_all(tiles, axes[k], split_axis=k, concat_axis=k, tiled=True)  34.2 us
    unnamed x13, local copies, waits for them, and re-layouts  23.6 us
    all_to_all x1, local copies, waits for them, and re-layouts, per_device(): lax.all_to_all(jnp.tile(arrived, repeats), 'tensor', split_axis=3, concat...  15.6 us
    dot_general x1, matrix products, per_device(): jnp.einsum('sjcf,jfd->sjcd', hidden, w_down, preferred_element_type=jnp.f...  11.5 us
    all_to_all x2, starting transfers between devices, sent_and_summed(): lax.all_to_all(tiles, axis, split_axis=0, concat_axis=0, tiled=True)  8.95 us
  transfers between devices with their start and end apart: 5, of which 4 were waited for; matrix products, arithmetic and copies ran while one was open for 16% of the time, Pallas kernels for 0%

profile of v1, /device:TPU:32, one launch (start us, length us, event | category | flops | bytes accessed | tf_op | source)
XLA Modules:
  0.0 371.1 jit_solution(17866235579679472113)
XLA Ops:
  0.0 0.8 convert_reduce_fusion.1
  0.9 0.2 reduce_window_sum.11
  1.2 0.7 select_reduce_fusion
  1.9 0.7 compare_select_fusion.2
  2.6 0.1 copy.51
  2.7 0.1 reshape.101
  3.0 2.4 scatter_custom_fusion
  5.4 1.0 concatenate.3
  6.4 2.8 gather_fusion
  9.2 1.4 reshape.103
  10.6 56.1 %all_to_all.35 = bf16[64,12,896]{2,1,0:T(8,128)(2,1)} all-to-all(bf16[64,12,896]{2,1,0:T(8,128)(2,1)} %reshape.103), channel_id=1, replica_groups=mesh['expert_0'=4,'expert_1'=8,'expert_2'=2,'tensor'=4] {'expert_0','exp..., dimensions={0} | all-to-all | bytes 2752512 | tf_op jit(solution)/shard_map/all_to_all | solution.py:75
  66.8 8.0 %copy.52 = bf16[64,12,896]{0,1,2:T(8,128)(2,1)} copy(bf16[64,12,896]{2,1,0:T(8,128)(2,1)} %all_to_all.35) | data formatting | bytes 2752512 | tf_op jit(solution)/shard_map/all_to_all | solution.py:75
  74.8 8.6 %tile.8 = bf16[64,12,4,896]{0,1,3,2:T(8,128)(2,1)} broadcast(bf16[64,12,896]{0,1,2:T(8,128)(2,1)} %copy.52), dimensions={0,1,3} | broadcast | bytes 6881280 | tf_op jit(solution)/shard_map/tile | solution.py:80
  83.4 11.6 %reshape.145 = bf16[4,2,344064]{2,1,0:T(2,128)(2,1)} reshape(bf16[3584,1,12,64]{3,2,1,0:T(8,128)(2,1)} %bitcast.101) | data formatting | bytes 11010048
  95.0 5.2 %all-to-all-start.1 = ((bf16[4,2,344064]{2,1,0:T(2,128)(2,1)}), bf16[4,2,344064]{2,1,0:T(2,128)(2,1)}, u32[]{:S(2)}, u32[]{:S(2)}) async-start(bf16[4,2,344064]{2,1,0:T(2,128)(2,1)} %reshape.145), calls=%async_computation.1 | async-start | bytes 11010048 | tf_op jit(solution)/shard_map/all_to_all | solution.py:79
  100.2 0.2 copy.61
  100.4 63.3 %all-to-all-done.1 = bf16[4,2,344064]{2,1,0:T(2,128)(2,1)} async-done(((bf16[4,2,344064]{2,1,0:T(2,128)(2,1)}), bf16[4,2,344064]{2,1,0:T(2,128)(2,1)}, u32[]{:S(2)}, u32[]{:S(2)}) %all-to-all-start.1) | async-done | bytes 5505056 | tf_op jit(solution)/shard_map/all_to_all | solution.py:79
  163.7 1.0 broadcast_in_dim.25
  164.7 3.7 all-to-all-start.5
  168.4 11.8 %reshape.146 = bf16[3584,1,12,64]{3,2,1,0:T(8,128)(2,1)} reshape(bf16[4,2,344064]{2,1,0:T(2,128)(2,1)} %all-to-all-done.1) | data formatting | bytes 11010048
  180.2 15.6 %copy.53 = bf16[64,1,12,3584]{3,0,2,1:T(8,128)(2,1)} copy(bf16[64,1,12,3584]{0,2,1,3:T(8,128)(2,1)} %bitcast.100) | data formatting | bytes 11010048 | tf_op jit(solution)/shard_map/all_to_all | solution.py:79
  195.8 5.6 %fusion.7 = f32[64,1,12,256]{3,0,2,1:T(8,128)} fusion(bf16[1,3584,256]{2,1,0:T(8,128)(2,1)} %param.12, bf16[64,1,12,3584]{3,0,2,1:T(8,128)(2,1)} %copy.53), kind=kOutput, calls=%fused_computation.16 | convolution fusion | flops 1409286144 | bytes 8126464 | tf_op jit(solution)/shard_map/sjcd,jdf->sjcf/dot_general | solution.py:82
  201.5 11.5 %convolution_convert_fusion = bf16[64,12,3584]{2,0,1:T(8,128)(2,1)} fusion(bf16[1,256,3584]{2,1,0:T(8,128)(2,1)S(1)} %copy-done, bf16[1,3584,256]{2,1,0:T(8,128)(2,1)} %param.13, bf16[64,1,12,3584]{3,0,2,1:T(8,128)(2,1)} %copy.53, f32[64,1,12,256]{3,0,2,1:T(8,128)} %fusion.7), kind=kOutput, calls=%fused_computation.3 | convolution fusion | flops 2822504448 | bytes 15466496 | tf_op jit(solution)/shard_map/sjcf,jfd->sjcd/dot_general | solution.py:85
  212.9 5.9 %copy.69 = bf16[1,12,8,4,8,896]{5,4,2,1,0,3:T(8,128)(2,1)} copy(bf16[1,12,8,4,8,896]{5,4,3,2,1,0:T(8,128)(2,1)} %bitcast.105) | data formatting | bytes 11010048 | tf_op jit(solution)/shard_map/reshape | solution.py:27
  218.8 5.2 %all-to-all-start.2 = ((bf16[4,64,1,12,896]{4,1,3,2,0:T(8,128)(2,1)}), bf16[4,64,1,12,896]{4,1,3,2,0:T(8,128)(2,1)}, u32[]{:S(2)}, u32[]{:S(2)}) async-start(bf16[4,64,1,12,896]{4,1,3,2,0:T(8,128)(2,1)} %bitcast.102), calls=%async_computation.2 | async-start | bytes 11010048 | tf_op jit(solution)/shard_map/all_to_all | solution.py:32
  224.1 0.5 fusion.53
  224.5 3.3 convolution_convert_fusion.1
  227.8 1.0 copy.70
  228.8 57.8 %all-to-all-done.2 = bf16[4,64,1,12,896]{4,1,3,2,0:T(8,128)(2,1)} async-done(((bf16[4,64,1,12,896]{4,1,3,2,0:T(8,128)(2,1)}), bf16[4,64,1,12,896]{4,1,3,2,0:T(8,128)(2,1)}, u32[]{:S(2)}, u32[]{:S(2)}) %all-to-all-start.2) | async-done | bytes 5505056 | tf_op jit(solution)/shard_map/all_to_all | solution.py:32
  286.7 3.6 reduce_sum.50
  290.2 0.6 convert_element_type.59
  290.8 0.2 copy.56
  291.0 4.8 %all_to_all.36 = bf16[32,2,1,12,896]{4,0,3,2,1:T(8,128)(2,1)S(1)} all-to-all(bf16[32,2,1,12,896]{4,0,3,2,1:T(8,128)(2,1)S(1)} %copy.56), channel_id=1, replica_groups=mesh['expert_0'=4,'expert_1'=8,'expert_2'=2,'tensor'=4] {'expert_2'}, dimensions={1} | all-to-all | bytes 2752512 | tf_op jit(solution)/shard_map/all_to_all | solution.py:40
  295.8 3.7 %all-to-all-start.6 = ((bf16[4,128,896]{2,1,0:T(8,128)(2,1)}), bf16[4,128,896]{2,1,0:T(8,128)(2,1)S(1)}, u32[]{:S(2)}, u32[]{:S(2)}) async-start(bf16[4,128,896]{2,1,0:T(8,128)(2,1)} %bitcast.99), calls=%async_computation.6 | async-start | bytes 1835008 | tf_op jit(solution)/shard_map/all_to_all | solution.py:32
  299.6 2.5 copy.57
  302.1 11.5 %all-to-all-done.6 = bf16[4,128,896]{2,1,0:T(8,128)(2,1)S(1)} async-done(((bf16[4,128,896]{2,1,0:T(8,128)(2,1)}), bf16[4,128,896]{2,1,0:T(8,128)(2,1)S(1)}, u32[]{:S(2)}, u32[]{:S(2)}) %all-to-all-start.6) | async-done | bytes 917536 | tf_op jit(solution)/shard_map/all_to_all | solution.py:32
  313.6 7.2 %all-to-all-start.4 = ((bf16[32,2,1,12,896]{4,1,3,2,0:T(2,128)(2,1)}), bf16[32,2,1,12,896]{4,1,3,2,0:T(2,128)(2,1)S(1)}, u32[]{:S(2)}, u32[]{:S(2)}) async-start(bf16[32,2,1,12,896]{4,1,3,2,0:T(2,128)(2,1)} %copy.57), calls=%async_computation.4 | async-start | bytes 2752512 | tf_op jit(solution)/shard_map/all_to_all | solution.py:40
  320.7 0.1 copy.60
  321.0 0.1 copy.47
  321.1 0.1 convert_reduce_fusion
  321.2 34.2 %all-to-all-done.4 = bf16[32,2,1,12,896]{4,1,3,2,0:T(2,128)(2,1)S(1)} async-done(((bf16[32,2,1,12,896]{4,1,3,2,0:T(2,128)(2,1)}), bf16[32,2,1,12,896]{4,1,3,2,0:T(2,128)(2,1)S(1)}, u32[]{:S(2)}, u32[]{:S(2)}) %all-to-all-start.4) | async-done | bytes 1376288 | tf_op jit(solution)/shard_map/all_to_all | solution.py:40
  355.4 0.3 copy_convert_fusion
  355.8 3.4 copy.59
  359.2 2.9 reshape.112
  362.1 2.7 gather_fusion.1
  364.8 2.9 reshape.122
  367.7 2.7 multiply_reduce_fusion
  370.4 0.7 add_convert_fusion
  (21 shorter events, 0.4 us)
Async XLA Ops:
  0.0 201.5 %copy-start = (bf16[1,256,3584]{2,1,0:T(8,128)(2,1)S(1)}, bf16[1,256,3584]{2,1,0:T(8,128)(2,1)}, u32[]{:S(2)}) copy-start(bf16[1,256,3584]{2,1,0:T(8,128)(2,1)} %param.14) | copy-start | bytes 5505028
  95.0 5.3 %copy-start.3 = (bf16[128,896]{1,0:T(8,128)(2,1)S(1)}, bf16[128,896]{1,0:T(8,128)(2,1)}, u32[]{:S(2)}) copy-start(bf16[128,896]{1,0:T(8,128)(2,1)} %param.9) | copy-start | bytes 688132
  95.0 68.7 %all-to-all-start.1 = ((bf16[4,2,344064]{2,1,0:T(2,128)(2,1)}), bf16[4,2,344064]{2,1,0:T(2,128)(2,1)}, u32[]{:S(2)}, u32[]{:S(2)}) async-start(bf16[4,2,344064]{2,1,0:T(2,128)(2,1)} %reshape.145), calls=%async_computation.1 | async-start | bytes 11010048 | tf_op jit(solution)/shard_map/all_to_all | solution.py:79
  164.7 54.1 %all-to-all-start.5 = ((bf16[4,128,896]{1,2,0:T(8,128)(2,1)}), bf16[4,128,896]{1,2,0:T(8,128)(2,1)S(1)}, u32[]{:S(2)}, u32[]{:S(2)}) async-start(bf16[4,128,896]{1,2,0:T(8,128)(2,1)} %broadcast_in_dim.25), calls=%async_computation.5 | async-start | bytes 1835008 | tf_op jit(solution)/shard_map/all_to_all | solution.py:18
  218.8 5.2 %copy-start.2 = (bf16[3584,256]{1,0:T(8,128)(2,1)S(1)}, bf16[3584,256]{1,0:T(8,128)(2,1)}, u32[]{:S(2)}) copy-start(bf16[3584,256]{1,0:T(8,128)(2,1)} %param.15) | copy-start | bytes 5505028
  218.8 67.8 %all-to-all-start.2 = ((bf16[4,64,1,12,896]{4,1,3,2,0:T(8,128)(2,1)}), bf16[4,64,1,12,896]{4,1,3,2,0:T(8,128)(2,1)}, u32[]{:S(2)}, u32[]{:S(2)}) async-start(bf16[4,64,1,12,896]{4,1,3,2,0:T(8,128)(2,1)} %bitcast.102), calls=%async_computation.2 | async-start | bytes 11010048 | tf_op jit(solution)/shard_map/all_to_all | solution.py:32
  295.8 17.7 %all-to-all-start.6 = ((bf16[4,128,896]{2,1,0:T(8,128)(2,1)}), bf16[4,128,896]{2,1,0:T(8,128)(2,1)S(1)}, u32[]{:S(2)}, u32[]{:S(2)}) async-start(bf16[4,128,896]{2,1,0:T(8,128)(2,1)} %bitcast.99), calls=%async_computation.6 | async-start | bytes 1835008 | tf_op jit(solution)/shard_map/all_to_all | solution.py:32
  302.1 18.9 %copy-start.4 = (bf16[128,4]{0,1:T(4,128)(2,1)S(1)}, bf16[128,4]{0,1:T(4,128)(2,1)}, u32[]{:S(2)}) copy-start(bf16[128,4]{0,1:T(4,128)(2,1)} %param.11) | copy-start | bytes 3076
  313.6 41.9 %all-to-all-start.4 = ((bf16[32,2,1,12,896]{4,1,3,2,0:T(2,128)(2,1)}), bf16[32,2,1,12,896]{4,1,3,2,0:T(2,128)(2,1)S(1)}, u32[]{:S(2)}, u32[]{:S(2)}) async-start(bf16[32,2,1,12,896]{4,1,3,2,0:T(2,128)(2,1)} %copy.57), calls=%async_computation.4 | async-start | bytes 2752512 | tf_op jit(solution)/shard_map/all_to_all | solution.py:40
  364.8 6.4 %copy-start.1 = (bf16[1,256,3584]{2,1,0:T(8,128)(2,1)S(1)}, bf16[1,256,3584]{2,1,0:T(8,128)(2,1)}, u32[]{:S(2)}) copy-start(bf16[1,256,3584]{2,1,0:T(8,128)(2,1)} %param.14) | copy-start | bytes 5505028
